TPU v7x, 32 devices: a whole 2x2x4 slice. The times are simulated.
32 devices in a mesh: bank: 4 (over y, x), zero: 8 (over z, core).
Axes of the slice: x: 2, y: 2, z: 4, core: 2. Of those that a mesh axis runs over, the one named last changes fastest.
Arguments:
- master_gate: float32 [64, 2048, 1024], P('bank', 'zero'), may hold values from -0.1875 to 0.1875
- master_up: float32 [64, 2048, 1024], P('bank', 'zero'), may hold values from -0.1875 to 0.1875
- master_down: float32 [64, 1024, 2048], P('bank', None, 'zero'), may hold values from -0.25 to 0.25
- router_weight: float32 [2048, 64], P('zero', 'bank'), may hold values from -0.125 to 0.125
- router_gain: float32 [2048], P('zero'), may hold values from 0.25 to 1.75
Outputs:
- final_gate: bfloat16 [64, 2048, 1024], P('bank', None, 'zero')
- final_up: bfloat16 [64, 2048, 1024], P('bank', None, 'zero')
- final_down: bfloat16 [64, 1024, 2048], P('bank', 'zero')
- scale_gate: float32 [64, 1024], P('bank', 'zero')
- scale_up: float32 [64, 1024], P('bank', 'zero')
- scale_down: float32 [64, 1024], P('bank', 'zero')
- serve_router: bfloat16 [2048, 64], replicated
All inputs are finite; a program needn't handle non-finite values.
Results may differ from a plain program's by a relative error of at most 0.0085.
Values may be sent and summed in bfloat16 or wider, within the bound.
A program may use at most 192 MiB of HBM per device.

v0:
```python
import jax
import jax.numpy as jnp
from jax import lax
from jax.sharding import PartitionSpec as P


def local(master_gate, master_up, master_down, router_weight, router_gain):
    total_gate, total_up, total_down = (
        lax.psum(jnp.sum(master_gate * master_gate, axis=1).astype(jnp.bfloat16), "zero").astype(
            jnp.float32
        ),
        lax.psum(jnp.sum(master_up * master_up, axis=1).astype(jnp.bfloat16), "zero").astype(
            jnp.float32
        ),
        lax.psum(jnp.sum(master_down * master_down, axis=2).astype(jnp.bfloat16), "zero").astype(
            jnp.float32
        ),
    )
    scale_gate = jnp.sqrt(total_gate)
    scale_up = jnp.sqrt(total_up)
    scale_down = jnp.sqrt(total_down)
    narrow_gate, narrow_up, narrow_down = (
        (master_gate / jnp.expand_dims(scale_gate, 1)).astype(jnp.bfloat16),
        (master_up / jnp.expand_dims(scale_up, 1)).astype(jnp.bfloat16),
        (master_down / jnp.expand_dims(scale_down, 2)).astype(jnp.bfloat16),
    )
    final_gate, final_up = (
        lax.all_to_all(narrow_gate, "zero", split_axis=2, concat_axis=1, tiled=True),
        lax.all_to_all(narrow_up, "zero", split_axis=2, concat_axis=1, tiled=True),
    )
    final_down = lax.all_to_all(narrow_down, "zero", split_axis=1, concat_axis=2, tiled=True)
    scale_gate = lax.dynamic_slice_in_dim(
        scale_gate, lax.axis_index("zero") * final_gate.shape[2], final_gate.shape[2], axis=1
    )
    scale_up = lax.dynamic_slice_in_dim(
        scale_up, lax.axis_index("zero") * final_up.shape[2], final_up.shape[2], axis=1
    )
    scale_down = lax.dynamic_slice_in_dim(
        scale_down, lax.axis_index("zero") * final_down.shape[1], final_down.shape[1], axis=1
    )
    part_router = (router_weight * router_gain[:, None]).astype(jnp.bfloat16)
    row_router = lax.all_gather(part_router, "zero", axis=0, tiled=True)
    serve_router = lax.all_gather(row_router, "bank", axis=1, tiled=True)
    return (final_gate, final_up, final_down, scale_gate, scale_up, scale_down, serve_router)


def solution(mesh):
    in_specs = (
        P("bank", "zero", None),
        P("bank", "zero", None),
        P("bank", None, "zero"),
        P("zero", "bank"),
        P("zero"),
    )
    out_specs = (
        P("bank", None, "zero"),
        P("bank", None, "zero"),
        P("bank", "zero", None),
        P("bank", "zero"),
        P("bank", "zero"),
        P("bank", "zero"),
        P(),
    )
    return jax.shard_map(local, mesh=mesh, in_specs=in_specs, out_specs=out_specs, check_vma=False)
```

profile of v0, /device:TPU:0, one launch (start us, length us, event | category | flops | bytes accessed | tf_op | source)
XLA Modules:
  0.0 735.5 jit_solution(5849553239069995700)
XLA Ops:
  7.2 0.0 all-reduce.3.cloned.1.call-start
  7.2 8.6 %multiply_reduce_fusion = bf16[16,1024]{1,0:T(8,128)(2,1)} fusion(f32[16,1024,256]{2,1,0:T(8,128)} %param.7), kind=kLoop, calls=%fused_computation.2 | loop fusion | flops 8372224 | bytes 16809984 | tf_op jit(solution)/shard_map/reduce_sum | solution.py:15
  15.8 12.5 %multiply_reduce_fusion.1 = (bf16[16,1024]{1,0:T(8,128)(2,1)}, bf16[16,1024]{1,0:T(8,128)(2,1)}) fusion(f32[16,256,1024]{2,1,0:T(8,128)} %param.6, f32[16,256,1024]{2,1,0:T(8,128)} %param.5), kind=kLoop, calls=%fused_computation.4 | loop fusion | flops 16744448 | bytes 33619968 | tf_op jit(solution)/shard_map/reduce_sum | solution.py:12
  28.4 0.0 all-reduce.3.cloned.1.call-update
  28.4 17.6 %copy.19 = f32[16,256,1024]{1,0,2:T(8,128)} copy(f32[16,256,1024]{2,1,0:T(8,128)} %param.6) | data formatting | bytes 33554432 | tf_op args[1]
  46.0 37.9 %all-reduce.3.cloned.1.call-done = (bf16[16,1024]{1,0:T(8,128)(2,1)}, bf16[16,1024]{1,0:T(8,128)(2,1)}, bf16[16,1024]{1,0:T(8,128)(2,1)}) async-done(((bf16[16,1024]{1,0:T(8,128)(2,1)}, bf16[16,1024]{1,0:T(8,128)(2,1)}, bf16[16,1024]{1,0:T(8,128)(2,1)}), (bf16[16,1024]{1,0:T(8,128)(2,1)}, bf16[16,1024]{1,0:T(8,128)(2,1)}, bf16[16,1024]{1,0:T(8,128)(2,1)})) %all-reduce.3.cloned.1.call-update) | async-done | bytes 98320 | tf_op jit(solution)/shard_map/psum | solution.py:9
  84.0 0.8 convert_sqrt_fusion.1
  84.8 0.2 copy.18
  85.0 9.6 %divide_convert_fusion = bf16[16,256,1024]{1,0,2:T(8,128)(2,1)} fusion(f32[16,256,1024]{1,0,2:T(8,128)} %copy.19, f32[16,1024]{0,1:T(8,128)S(1)} %copy.18), kind=kLoop, calls=%fused_computation.3 | loop fusion | flops 8388608 | bytes 25231360 | tf_op jit(solution)/shard_map/convert_element_type | solution.py:24
  94.6 5.3 all-to-all-start.1
  99.9 0.0 copy-start.1
  99.9 17.6 %copy.16 = f32[16,256,1024]{1,0,2:T(8,128)} copy(f32[16,256,1024]{2,1,0:T(8,128)} %param.5) | data formatting | bytes 33554432 | tf_op args[0]
  117.5 0.0 copy-done.1
  117.6 0.2 copy.15
  117.8 0.0 copy-start
  117.8 9.6 %divide_convert_fusion.1 = bf16[16,256,1024]{1,0,2:T(8,128)(2,1)} fusion(f32[16,256,1024]{1,0,2:T(8,128)} %copy.16, f32[16,1024]{0,1:T(8,128)S(1)} %copy.15), kind=kLoop, calls=%fused_computation.5 | loop fusion | flops 8388608 | bytes 25231360 | tf_op jit(solution)/shard_map/convert_element_type | solution.py:23
  127.4 156.5 %all-to-all-done.1 = bf16[16,256,1024]{1,0,2:T(8,128)(2,1)} async-done(((bf16[16,256,1024]{1,0,2:T(8,128)(2,1)}), bf16[16,256,1024]{1,0,2:T(8,128)(2,1)}, u32[]{:S(2)}, u32[]{:S(2)}) %all-to-all-start.1) | async-done | bytes 8388640 | tf_op jit(solution)/shard_map/all_to_all | solution.py:29
  283.9 4.9 all-to-all-start
  288.9 0.0 copy-done
  288.9 0.2 copy.21
  289.1 0.0 copy-start.2
  289.1 0.0 copy-start.3
  289.1 16.6 %fusion = bf16[16,1024,256]{2,0,1:T(8,128)(2,1)} fusion(f32[16,1024,256]{2,1,0:T(8,128)} %param.7, f32[16,1024]{0,1:T(8,128)S(1)} %copy.21), kind=kLoop, calls=%fused_computation.1 | loop fusion | flops 8388608 | bytes 25231360 | tf_op jit(solution)/shard_map/convert_element_type | solution.py:25
  305.8 167.0 %all-to-all-done = bf16[16,256,1024]{1,0,2:T(8,128)(2,1)} async-done(((bf16[16,256,1024]{1,0,2:T(8,128)(2,1)}), bf16[16,256,1024]{1,0,2:T(8,128)(2,1)}, u32[]{:S(2)}, u32[]{:S(2)}) %all-to-all-start) | async-done | bytes 8388640 | tf_op jit(solution)/shard_map/all_to_all | solution.py:28
  472.7 5.0 all-to-all-start.2
  477.7 0.0 copy-done.2
  477.7 0.0 copy-done.3
  477.8 189.9 %all_gather.6 = bf16[2048,16]{0,1:T(8,128)(2,1)S(1)} all-gather(bf16[256,16]{0,1:T(8,128)(2,1)S(1)} %multiply_convert_fusion), channel_id=1, replica_groups=mesh['bank'=4,'zero'=8] {'zero'}, dimensions={0}, use_global_device_ids=true | all-gather | bytes 73728 | tf_op jit(solution)/shard_map/all_gather | solution.py:42
  667.6 9.1 %all_gather.7 = bf16[2048,64]{0,1:T(8,128)(2,1)S(1)} all-gather(bf16[2048,16]{0,1:T(8,128)(2,1)S(1)} %all_gather.6), channel_id=1, replica_groups=mesh['bank'=4,'zero'=8] {'bank'}, dimensions={1}, use_global_device_ids=true | all-gather | bytes 327680 | tf_op jit(solution)/shard_map/all_gather | solution.py:43
  676.8 0.6 constant_dynamic-slice_fusion
  677.4 0.6 constant_dynamic-slice_fusion.1
  678.0 0.6 constant_dynamic-slice_fusion.2
  678.6 12.3 %copy.20 = bf16[16,8,256,128]{3,2,1,0:T(8,128)(2,1)} copy(bf16[16,8,256,128]{2,0,3,1:T(8,128)(2,1)} %bitcast.4) | data formatting | bytes 16777216 | tf_op jit(solution)/shard_map/all_to_all | solution.py:29
  690.8 12.3 %copy.17 = bf16[16,8,256,128]{3,2,1,0:T(8,128)(2,1)} copy(bf16[16,8,256,128]{2,0,3,1:T(8,128)(2,1)} %bitcast.1) | data formatting | bytes 16777216 | tf_op jit(solution)/shard_map/all_to_all | solution.py:28
  703.1 0.0 all-to-all-done.2
  703.1 11.4 %copy.23 = bf16[16,128,8,256]{3,2,1,0:T(8,128)(2,1)} copy(bf16[16,128,8,256]{3,0,1,2:T(8,128)(2,1)} %bitcast.7) | data formatting | bytes 16777216 | tf_op jit(solution)/shard_map/all_to_all | solution.py:31
  714.5 13.4 %all_to_all.50 = bf16[16,128,2048]{2,1,0:T(8,128)(2,1)} reshape(bf16[16,128,8,256]{3,2,1,0:T(8,128)(2,1)} %copy.23) | data formatting | bytes 16777216 | tf_op jit(solution)/shard_map/all_to_all | solution.py:31
  727.9 0.7 copy.31
  (3 shorter events, 0.1 us)
Async XLA Ops:
  7.2 76.8 %all-reduce.3.cloned.1.call-start = ((), (), s32[]{:S(2)}) async-start(), calls=%async_computation.3 | async-start | bytes 196608 | tf_op jit(solution)/shard_map/psum | solution.py:9
  94.6 189.3 %all-to-all-start.1 = ((bf16[16,256,1024]{1,0,2:T(8,128)(2,1)}), bf16[16,256,1024]{1,0,2:T(8,128)(2,1)}, u32[]{:S(2)}, u32[]{:S(2)}) async-start(bf16[16,256,1024]{1,0,2:T(8,128)(2,1)} %divide_convert_fusion), calls=%async_computation.1 | async-start | bytes 16777216 | tf_op jit(solution)/shard_map/all_to_all | solution.py:29
  99.9 17.6 %copy-start.1 = (bf16[16,1024]{1,0:T(8,128)(2,1)S(1)}, bf16[16,1024]{1,0:T(8,128)(2,1)}, u32[]{:S(2)}) copy-start(bf16[16,1024]{1,0:T(8,128)(2,1)} %get-tuple-element.7) | copy-start | bytes 98308
  117.8 171.1 %copy-start = (bf16[16,1024]{1,0:T(8,128)(2,1)S(1)}, bf16[16,1024]{1,0:T(8,128)(2,1)}, u32[]{:S(2)}) copy-start(bf16[16,1024]{1,0:T(8,128)(2,1)} %get-tuple-element.9) | copy-start | bytes 98308
  283.9 188.8 %all-to-all-start = ((bf16[16,256,1024]{1,0,2:T(8,128)(2,1)}), bf16[16,256,1024]{1,0,2:T(8,128)(2,1)}, u32[]{:S(2)}, u32[]{:S(2)}) async-start(bf16[16,256,1024]{1,0,2:T(8,128)(2,1)} %divide_convert_fusion.1), calls=%async_computation | async-start | bytes 16777216 | tf_op jit(solution)/shard_map/all_to_all | solution.py:28
  289.1 188.6 %copy-start.2 = (f32[256,16]{0,1:T(8,128)S(1)}, f32[256,16]{0,1:T(8,128)}, u32[]{:S(2)}) copy-start(f32[256,16]{0,1:T(8,128)} %param.8) | copy-start | bytes 49156
  289.1 188.6 %copy-start.3 = (f32[256]{0:T(256)S(1)}, f32[256]{0:T(256)}, u32[]{:S(2)}) copy-start(f32[256]{0:T(256)} %param.9) | copy-start | bytes 3076
  472.7 230.4 %all-to-all-start.2 = ((bf16[16,1024,256]{2,0,1:T(8,128)(2,1)}), bf16[16,1024,256]{2,0,1:T(8,128)(2,1)}, u32[]{:S(2)}, u32[]{:S(2)}) async-start(bf16[16,1024,256]{2,0,1:T(8,128)(2,1)} %fusion), calls=%async_computation.2 | async-start | bytes 16777216 | tf_op jit(solution)/shard_map/all_to_all | solution.py:31
Sparse Core Ops, SparseCore 0:
  28.5 55.3 all-reduce.2
where the time goes:
time: 737 us; the launch traced here: 735 us
  waiting for transfers between devices  361 us (49%)
  blocking collectives  199 us (27%)
  local copies, waits for them, and re-layouts  87.7 us (12%)
  other arithmetic  57.9 us (8%)
  starting transfers between devices  15.3 us (2%)
  between operations  14.2 us (2%)
    all_gather x1, blocking collectives, local(): row_router = lax.all_gather(part_router, 'zero', axis=0, tiled=True)  190 us
    all_to_all x1, waiting for transfers between devices, local(): lax.all_to_all(narrow_gate, 'zero', split_axis=2, concat_axis=1, tiled=True)  167 us
    all_to_all x1, waiting for transfers between devices, local(): lax.all_to_all(narrow_up, 'zero', split_axis=2, concat_axis=1, tiled=True)  156 us
    psum x1, waiting for transfers between devices, local(): lax.psum(jnp.sum(master_gate * master_gate, axis=1).astype(jnp.bfloat16),...  37.9 us
    unnamed x11, local copies, waits for them, and re-layouts  35.9 us
    all_to_all x2, local copies, waits for them, and re-layouts, local(): lax.all_to_all(narrow_down, 'zero', split_axis=1, concat_axis=2, tiled=True)  24.8 us
    convert_element_type x1, other arithmetic, local(): (master_down / jnp.expand_dims(scale_down, 2)).astype(jnp.bfloat16)  16.6 us
  transfers between devices with their start and end apart: 4, of which 3 were waited for; matrix products, arithmetic and copies ran while one was open for 12% of the time, Pallas kernels for 0%

commit v1 on v0

--- a/solution.py
+++ b/solution.py
@@ -6,9 +6,10 @@
 
 def local(master_gate, master_up, master_down, router_weight, router_gain):
     total_gate, total_up, total_down = (
-        lax.psum(jnp.sum(master_gate * master_gate, axis=1).astype(jnp.bfloat16), "zero").astype(
-            jnp.float32
-        ),
+        jnp.sum(
+            lax.all_gather(jnp.sum(master_gate * master_gate, axis=1).astype(jnp.bfloat16), "zero"),
+            axis=0,
+        ).astype(jnp.float32),
         lax.psum(jnp.sum(master_up * master_up, axis=1).astype(jnp.bfloat16), "zero").astype(
             jnp.float32
         ),

time: 737 us -> 702 us (0.953)
  waiting for transfers between devices: 361 us -> 306 us
  blocking collectives: 199 us -> 215 us
    all_to_all x1, waiting for transfers between devices: 167 us -> 100 us  [local(): lax.all_to_all(narrow_gate, 'zero', split_axis=2, concat_axis=1, tiled=True)]
    all_gather x0 -> x1, blocking collectives: none -> 15.9 us  [local(): lax.all_gather(jnp.sum(master_gate * master_gate, axis=1).astype(jnp.bflo...]
    all_to_all x1, waiting for transfers between devices: 156 us -> 167 us  [local(): lax.all_to_all(narrow_up, 'zero', split_axis=2, concat_axis=1, tiled=True)]
    reduce_sum x0 -> x2, other arithmetic: none -> 8.04 us  [the longest x1 7.99 us: local(): jnp.sum(master_gate * master_gate, axis=1).astype(jnp.bfloat16)]
    unnamed x11 -> x9, local copies, waits for them, and re-layouts: 35.9 us -> 35.9 us
  transfers between devices with their start and end apart: 4 -> 4, of which waited for: 3 -> 3; matrix products, arithmetic and copies ran while one was open for 12% -> 13% of each run, Pallas kernels for 0% -> 0%
where the time goes in v1:
time: 702 us; the launch traced here: 700 us
  waiting for transfers between devices  306 us (44%)
  blocking collectives  215 us (31%)
  local copies, waits for them, and re-layouts  87 us (12%)
  other arithmetic  62 us (9%)
  starting transfers between devices  15.2 us (2%)
  between operations  14.2 us (2%)
    all_gather x1, blocking collectives, local(): row_router = lax.all_gather(part_router, 'zero', axis=0, tiled=True)  190 us
    all_to_all x1, waiting for transfers between devices, local(): lax.all_to_all(narrow_up, 'zero', split_axis=2, concat_axis=1, tiled=True)  167 us
    all_to_all x1, waiting for transfers between devices, local(): lax.all_to_all(narrow_gate, 'zero', split_axis=2, concat_axis=1, tiled=True)  100 us
    psum x1, waiting for transfers between devices, local(): lax.psum(jnp.sum(master_up * master_up, axis=1).astype(jnp.bfloat16), 'ze...  39.2 us
    unnamed x9, local copies, waits for them, and re-layouts  35.9 us
    all_to_all x2, local copies, waits for them, and re-layouts, local(): lax.all_to_all(narrow_down, 'zero', split_axis=1, concat_axis=2, tiled=True)  24.8 us
    convert_element_type x1, other arithmetic, local(): (master_down / jnp.expand_dims(scale_down, 2)).astype(jnp.bfloat16)  16.6 us
    all_gather x1, blocking collectives, local(): lax.all_gather(jnp.sum(master_gate * master_gate, axis=1).astype(jnp.bflo...  15.9 us
  transfers between devices with their start and end apart: 4, of which 3 were waited for; matrix products, arithmetic and copies ran while one was open for 13% of the time, Pallas kernels for 0%

profile of v1, /device:TPU:0, one launch (start us, length us, event | category | flops | bytes accessed | tf_op | source)
XLA Modules:
  0.0 699.5 jit_solution(17125554464032280629)
XLA Ops:
  7.2 17.6 %copy.25 = f32[16,256,1024]{1,0,2:T(8,128)} copy(f32[16,256,1024]{2,1,0:T(8,128)} %param.5) | data formatting | bytes 33554432 | tf_op args[0]
  24.7 8.0 %multiply_reduce_fusion.2 = bf16[16,1024]{1,0:T(8,128)(2,1)S(1)} fusion(f32[16,256,1024]{2,1,0:T(8,128)} %param.5), kind=kLoop, calls=%fused_computation.6 | loop fusion | flops 8372224 | bytes 16809984 | tf_op jit(solution)/shard_map/reduce_sum | solution.py:10
  32.7 15.9 %all-gather = bf16[128,1024]{1,0:T(8,128)(2,1)S(1)} all-gather(bf16[16,1024]{1,0:T(8,128)(2,1)S(1)} %multiply_reduce_fusion.2), channel_id=2, replica_groups=mesh['bank'=4,'zero'=8] {'zero'}, dimensions={0}, use_global_device_ids=true | all-gather | bytes 294912 | tf_op jit(solution)/shard_map/all_gather | solution.py:10
  48.7 0.2 copy.24
  48.9 9.6 %divide_convert_fusion.1 = bf16[16,256,1024]{1,0,2:T(8,128)(2,1)} fusion(f32[16,256,1024]{1,0,2:T(8,128)} %copy.25, f32[16,1024]{0,1:T(8,128)S(1)} %copy.24), kind=kLoop, calls=%fused_computation.5 | loop fusion | flops 8388608 | bytes 25231360 | tf_op jit(solution)/shard_map/convert_element_type | solution.py:24
  58.6 5.0 all-to-all-start
  63.6 0.0 all-reduce.3.cloned.1.call-start
  63.6 8.6 %multiply_reduce_fusion.1 = bf16[16,1024]{1,0:T(8,128)(2,1)} fusion(f32[16,256,1024]{2,1,0:T(8,128)} %param.6), kind=kLoop, calls=%fused_computation.4 | loop fusion | flops 8372224 | bytes 16809984 | tf_op jit(solution)/shard_map/reduce_sum | solution.py:13
  72.2 8.6 %multiply_reduce_fusion = bf16[16,1024]{1,0:T(8,128)(2,1)} fusion(f32[16,1024,256]{2,1,0:T(8,128)} %param.7), kind=kLoop, calls=%fused_computation.2 | loop fusion | flops 8372224 | bytes 16809984 | tf_op jit(solution)/shard_map/reduce_sum | solution.py:16
  80.8 0.0 all-reduce.3.cloned.1.call-update
  80.9 17.6 %copy.28 = f32[16,256,1024]{1,0,2:T(8,128)} copy(f32[16,256,1024]{2,1,0:T(8,128)} %param.6) | data formatting | bytes 33554432 | tf_op args[1]
  98.5 39.2 %all-reduce.3.cloned.1.call-done = (bf16[16,1024]{1,0:T(8,128)(2,1)}, bf16[16,1024]{1,0:T(8,128)(2,1)}) async-done(((bf16[16,1024]{1,0:T(8,128)(2,1)}, bf16[16,1024]{1,0:T(8,128)(2,1)}), (bf16[16,1024]{1,0:T(8,128)(2,1)}, bf16[16,1024]{1,0:T(8,128)(2,1)})) %all-reduce.3.cloned.1.call-update) | async-done | bytes 65552 | tf_op jit(solution)/shard_map/psum | solution.py:13
  137.7 0.8 convert_sqrt_fusion.1
  138.5 0.2 copy.27
  138.7 0.0 copy-start
  138.7 9.6 %divide_convert_fusion = bf16[16,256,1024]{1,0,2:T(8,128)(2,1)} fusion(f32[16,256,1024]{1,0,2:T(8,128)} %copy.28, f32[16,1024]{0,1:T(8,128)S(1)} %copy.27), kind=kLoop, calls=%fused_computation.3 | loop fusion | flops 8388608 | bytes 25231360 | tf_op jit(solution)/shard_map/convert_element_type | solution.py:25
  148.3 100.3 %all-to-all-done = bf16[16,256,1024]{1,0,2:T(8,128)(2,1)} async-done(((bf16[16,256,1024]{1,0,2:T(8,128)(2,1)}), bf16[16,256,1024]{1,0,2:T(8,128)(2,1)}, u32[]{:S(2)}, u32[]{:S(2)}) %all-to-all-start) | async-done | bytes 8388640 | tf_op jit(solution)/shard_map/all_to_all | solution.py:29
  248.6 5.1 all-to-all-start.1
  253.8 0.0 copy-done
  253.8 0.2 copy.30
  254.0 0.0 copy-start.1
  254.0 0.0 copy-start.2
  254.1 16.6 %fusion = bf16[16,1024,256]{2,0,1:T(8,128)(2,1)} fusion(f32[16,1024,256]{2,1,0:T(8,128)} %param.7, f32[16,1024]{0,1:T(8,128)S(1)} %copy.30), kind=kLoop, calls=%fused_computation.1 | loop fusion | flops 8388608 | bytes 25231360 | tf_op jit(solution)/shard_map/convert_element_type | solution.py:26
  270.7 166.8 %all-to-all-done.1 = bf16[16,256,1024]{1,0,2:T(8,128)(2,1)} async-done(((bf16[16,256,1024]{1,0,2:T(8,128)(2,1)}), bf16[16,256,1024]{1,0,2:T(8,128)(2,1)}, u32[]{:S(2)}, u32[]{:S(2)}) %all-to-all-start.1) | async-done | bytes 8388640 | tf_op jit(solution)/shard_map/all_to_all | solution.py:30
  437.5 5.0 all-to-all-start.2
  442.5 0.0 copy-done.1
  442.5 0.0 copy-done.2
  442.6 189.9 %all_gather.11 = bf16[2048,16]{0,1:T(8,128)(2,1)S(1)} all-gather(bf16[256,16]{0,1:T(8,128)(2,1)S(1)} %multiply_convert_fusion), channel_id=1, replica_groups=mesh['bank'=4,'zero'=8] {'zero'}, dimensions={0}, use_global_device_ids=true | all-gather | bytes 73728 | tf_op jit(solution)/shard_map/all_gather | solution.py:43
  632.4 9.0 %all_gather.12 = bf16[2048,64]{0,1:T(8,128)(2,1)S(1)} all-gather(bf16[2048,16]{0,1:T(8,128)(2,1)S(1)} %all_gather.11), channel_id=1, replica_groups=mesh['bank'=4,'zero'=8] {'bank'}, dimensions={1}, use_global_device_ids=true | all-gather | bytes 327680 | tf_op jit(solution)/shard_map/all_gather | solution.py:44
  641.4 0.6 constant_dynamic-slice_fusion.2
  642.0 0.6 constant_dynamic-slice_fusion
  642.6 12.3 %copy.26 = bf16[16,8,256,128]{3,2,1,0:T(8,128)(2,1)} copy(bf16[16,8,256,128]{2,0,3,1:T(8,128)(2,1)} %bitcast.2) | data formatting | bytes 16777216 | tf_op jit(solution)/shard_map/all_to_all | solution.py:29
  654.9 12.3 %copy.29 = bf16[16,8,256,128]{3,2,1,0:T(8,128)(2,1)} copy(bf16[16,8,256,128]{2,0,3,1:T(8,128)(2,1)} %bitcast.5) | data formatting | bytes 16777216 | tf_op jit(solution)/shard_map/all_to_all | solution.py:30
  667.2 0.0 all-to-all-done.2
  667.2 11.4 %copy.32 = bf16[16,128,8,256]{3,2,1,0:T(8,128)(2,1)} copy(bf16[16,128,8,256]{3,0,1,2:T(8,128)(2,1)} %bitcast.8) | data formatting | bytes 16777216 | tf_op jit(solution)/shard_map/all_to_all | solution.py:32
  678.6 13.4 %all_to_all.50 = bf16[16,128,2048]{2,1,0:T(8,128)(2,1)} reshape(bf16[16,128,8,256]{3,2,1,0:T(8,128)(2,1)} %copy.32) | data formatting | bytes 16777216 | tf_op jit(solution)/shard_map/all_to_all | solution.py:32
  692.0 0.7 copy.39
  (4 shorter events, 0.1 us)
Async XLA Ops:
  58.6 190.1 %all-to-all-start = ((bf16[16,256,1024]{1,0,2:T(8,128)(2,1)}), bf16[16,256,1024]{1,0,2:T(8,128)(2,1)}, u32[]{:S(2)}, u32[]{:S(2)}) async-start(bf16[16,256,1024]{1,0,2:T(8,128)(2,1)} %divide_convert_fusion.1), calls=%async_computation | async-start | bytes 16777216 | tf_op jit(solution)/shard_map/all_to_all | solution.py:29
  63.6 74.1 %all-reduce.3.cloned.1.call-start = ((), (), s32[]{:S(2)}) async-start(), calls=%async_computation.3 | async-start | bytes 131072 | tf_op jit(solution)/shard_map/psum | solution.py:13
  138.7 115.1 %copy-start = (bf16[16,1024]{1,0:T(8,128)(2,1)S(1)}, bf16[16,1024]{1,0:T(8,128)(2,1)}, u32[]{:S(2)}) copy-start(bf16[16,1024]{1,0:T(8,128)(2,1)} %get-tuple-element.8) | copy-start | bytes 98308
  248.6 188.8 %all-to-all-start.1 = ((bf16[16,256,1024]{1,0,2:T(8,128)(2,1)}), bf16[16,256,1024]{1,0,2:T(8,128)(2,1)}, u32[]{:S(2)}, u32[]{:S(2)}) async-start(bf16[16,256,1024]{1,0,2:T(8,128)(2,1)} %divide_convert_fusion), calls=%async_computation.1 | async-start | bytes 16777216 | tf_op jit(solution)/shard_map/all_to_all | solution.py:30
  254.0 188.5 %copy-start.1 = (f32[256,16]{0,1:T(8,128)S(1)}, f32[256,16]{0,1:T(8,128)}, u32[]{:S(2)}) copy-start(f32[256,16]{0,1:T(8,128)} %param.8) | copy-start | bytes 49156
  254.0 188.5 %copy-start.2 = (f32[256]{0:T(256)S(1)}, f32[256]{0:T(256)}, u32[]{:S(2)}) copy-start(f32[256]{0:T(256)} %param.9) | copy-start | bytes 3076
  437.5 229.7 %all-to-all-start.2 = ((bf16[16,1024,256]{2,0,1:T(8,128)(2,1)}), bf16[16,1024,256]{2,0,1:T(8,128)(2,1)}, u32[]{:S(2)}, u32[]{:S(2)}) async-start(bf16[16,1024,256]{2,0,1:T(8,128)(2,1)} %fusion), calls=%async_computation.2 | async-start | bytes 16777216 | tf_op jit(solution)/shard_map/all_to_all | solution.py:32
Sparse Core Ops, SparseCore 0:
  81.0 56.6 all-reduce.2
